TPU v7x, 32 devices: a whole 2x2x4 slice. The times are simulated.
32 devices in a mesh: dp: 8 (over z, x), vocab: 4 (over y, core).
Axes of the slice: x: 2, y: 2, z: 4, core: 2. Of those that a mesh axis runs over, the one named last changes fastest.
Arguments:
- hidden_states: bfloat16 [1024, 3584], P('dp', 'vocab'), may hold values from -750 to 750, as said below
- head_weight: bfloat16 [152064, 3584], P(('dp', 'vocab')), may hold values from -0.09375 to 0.09375
- token_ids: int32 [1024], P('dp'), may hold values from 0 to 152063
- response_mask: int32 [1024], P('dp'), may hold values 0 or 1
- rollout_logprobs: float32 [1024], P('dp'), may hold values from -14 to -6
- advantages: float32 [1024], P('dp'), may hold values from -6 to 6
Outputs:
- logprobs: float32 [1024], P('dp')
- tis_weight: float32 [1024], P('dp')
- loss: float32 [], replicated
Inputs may be any that keep to these rules, and one draw needn't show every extreme that they name: `hidden_states`: hidden states; some rows may be far larger than others.
All inputs are finite; a program needn't handle non-finite values. No bound on the sum of `response_mask` on one device may be relied on, other than what follows from the above.
Results may differ from a plain program's by a relative error of at most 0.0003.
Values may be sent and summed in bfloat16 or wider, within the bound.
A program may use at most 128 MiB of HBM per device.

v0:
```python
import jax
import jax.numpy as jnp
from jax import lax
from jax.sharding import PartitionSpec as P


def shard_stats(logits, ids_block, columns):
    matched = columns[None, :] == ids_block[:, None]
    picked = jnp.sum(jnp.where(matched, logits, 0.0), axis=1)
    peak = jnp.max(logits, axis=1)
    total = jnp.sum(jnp.exp(logits - peak[:, None]), axis=1)
    return (peak, total, picked)


def token_terms(logp, rollout, advant, mask):
    weight = jnp.minimum(jnp.exp(logp - rollout), 2.0)
    counted = mask.astype(jnp.float32)
    loss_part = -jnp.sum(counted * weight * advant * logp)
    return (weight, loss_part, jnp.sum(counted))


def body(hidden_states, head_weight, token_ids, response_mask, rollout_logprobs, advantages):
    rows_local = token_ids.shape[0]
    vocab_local = head_weight.shape[0]
    offset = lax.axis_index(("dp", "vocab")) * vocab_local
    own_columns = lax.iota(jnp.int32, vocab_local) + offset
    dp_index = lax.axis_index("dp")
    own_start = dp_index * rows_local
    all_ids, all_mask = (
        lax.all_gather(token_ids, "dp", axis=0, tiled=True),
        lax.all_gather(response_mask, "dp", axis=0, tiled=True),
    )
    all_rollout, all_advant = (
        lax.all_gather(rollout_logprobs, "dp", axis=0, tiled=True),
        lax.all_gather(advantages, "dp", axis=0, tiled=True),
    )
    full_rows = lax.all_gather(hidden_states, "vocab", axis=1, tiled=True)
    logits = jnp.einsum(
        "rd,vd->rv",
        lax.all_gather(full_rows, "dp", axis=0, tiled=True),
        head_weight,
        preferred_element_type=jnp.float32,
    )
    peak, total, picked = shard_stats(logits, all_ids, own_columns)
    peak, total, picked = (peak, total, picked)
    top = lax.pmax(peak, ("dp", "vocab"))
    total_sum, picked_sum = lax.psum((total * jnp.exp(peak - top), picked), ("dp", "vocab"))
    logprob_all = picked_sum - (top + jnp.log(total_sum))
    own_logp = lax.dynamic_slice_in_dim(logprob_all, own_start, rows_local, 0)
    weight_all, loss_sum, count = token_terms(logprob_all, all_rollout, all_advant, all_mask)
    weight = lax.dynamic_slice_in_dim(weight_all, own_start, rows_local, 0)
    loss = loss_sum / jnp.maximum(count, 1.0)
    return (own_logp, weight, loss)


def solution(mesh):
    placed = (P("dp", "vocab"), P(("dp", "vocab"), None), P("dp"), P("dp"), P("dp"), P("dp"))
    return jax.shard_map(
        body, mesh=mesh, in_specs=placed, out_specs=(P("dp"), P("dp"), P()), check_vma=False
    )
```

profile of v0, /device:TPU:0, one launch (start us, length us, event | category | flops | bytes accessed | tf_op | source)
XLA Modules:
  0.0 274.0 jit_solution(17611963197525337187)
XLA Ops:
  7.2 0.0 all-gather.6.cloned.1.call-start
  7.2 12.5 %all_gather.19 = bf16[128,3584]{1,0:T(8,128)(2,1)} all-gather(bf16[128,896]{1,0:T(8,128)(2,1)} %param.6), channel_id=1, replica_groups=mesh['dp'=8,'vocab'=4] {'vocab'}, dimensions={1}, use_global_device_ids=true | all-gather | bytes 1146880 | tf_op jit(solution)/shard_map/all_gather | solution.py:37
  19.7 0.0 all-gather.6.cloned.1.call-update
  19.7 21.4 %all-gather.2 = s32[8,1,128]{2,1,0:T(1,128)S(1)} all-gather(s32[1,1,128]{2,1,0:T(1,128)} %bitcast.15), channel_id=1, replica_groups=mesh['dp'=8,'vocab'=4] {'dp'}, dimensions={0}, use_global_device_ids=true | all-gather | bytes 4608 | tf_op jit(solution)/shard_map/all_gather | solution.py:31
  41.2 0.6 convert_reduce_fusion
  42.4 17.1 %all-gather = s32[8,1,128]{2,1,0:T(1,128)S(1)} all-gather(s32[1,1,128]{2,1,0:T(1,128)} %bitcast.16), channel_id=1, replica_groups=mesh['dp'=8,'vocab'=4] {'dp'}, dimensions={0}, use_global_device_ids=true | all-gather | bytes 4608 | tf_op jit(solution)/shard_map/all_gather | solution.py:30
  59.5 18.8 %all-gather.1 = f32[8,1,128]{2,1,0:T(1,128)S(1)} all-gather(f32[1,1,128]{2,1,0:T(1,128)} %bitcast.17), channel_id=1, replica_groups=mesh['dp'=8,'vocab'=4] {'dp'}, dimensions={0}, use_global_device_ids=true | all-gather | bytes 4608 | tf_op jit(solution)/shard_map/all_gather | solution.py:34
  78.3 17.3 %all-gather.3 = f32[8,1,128]{2,1,0:T(1,128)S(1)} all-gather(f32[1,1,128]{2,1,0:T(1,128)} %bitcast.18), channel_id=1, replica_groups=mesh['dp'=8,'vocab'=4] {'dp'}, dimensions={0}, use_global_device_ids=true | all-gather | bytes 4608 | tf_op jit(solution)/shard_map/all_gather | solution.py:35
  95.6 36.2 %all-gather.6.cloned.1.call-done = bf16[1024,3584]{1,0:T(8,128)(2,1)} async-done(((bf16[128,3584]{1,0:T(8,128)(2,1)}), bf16[1024,3584]{1,0:T(8,128)(2,1)}) %all-gather.6.cloned.1.call-update) | async-done | bytes 7340048 | tf_op jit(solution)/shard_map/all_gather | solution.py:40
  131.8 43.0 %fusion = (f32[1024]{0:T(1024)S(1)}, f32[1024,4752]{0,1:T(8,128)}) fusion(bf16[1024,3584]{1,0:T(8,128)(2,1)} %all-gather.6.cloned.1.call-done, bf16[4752,3584]{1,0:T(8,128)(2,1)} %param.7), kind=kOutput, calls=%fused_computation.8 | convolution fusion | flops 34884698112 | bytes 60870656 | tf_op jit(solution)/shard_map/rd,vd->rv/dot_general | solution.py:38
  174.8 38.4 %pmax.7 = f32[1024]{0:T(1024)S(1)} all-reduce(f32[1024]{0:T(1024)S(1)} %get-tuple-element.9), channel_id=1, replica_groups=mesh['dp'=8,'vocab'=4] {'dp','vocab'}, use_global_device_ids=true, to_apply=%region_3.4 | all-reduce | flops 1024 | bytes 8192 | tf_op jit(solution)/shard_map/pmax | solution.py:46
  213.1 9.5 %exponential_reduce_fusion = (f32[1024]{0:T(1024)S(1)}, f32[1024]{0:T(1024)S(1)}) fusion(f32[1024,4752]{0,1:T(8,128)} %get-tuple-element.10, f32[1024]{0:T(1024)S(1)} %get-tuple-element.9, s32[1024]{0:T(1024)S(1)} %bitcast.14, s32[4752]{0:T(1024)S(1)} %iota_add_fusion), kind=kLoop, calls=%fused_computation | loop fusion | flops 24328192 | bytes 19499584 | tf_op jit(solution)/shard_map/reduce_sum | solution.py:11
  222.7 40.8 %all-reduce = (f32[1024]{0:T(1024)S(1)}, f32[1024]{0:T(1024)S(1)}) all-reduce(f32[1024]{0:T(1024)S(1)} %get-tuple-element.4, f32[1024]{0:T(1024)S(1)} %exponential_multiply_fusion), channel_id=1, replica_groups=mesh['dp'=8,'vocab'=4] {'dp','vocab'}, use_global_device_ids=true, to_apply=%region_1.2 | all-reduce | flops 2048 | bytes 16384 | tf_op jit(solution)/shard_map/psum | solution.py:47
  263.5 0.6 multiply_reduce_fusion
  264.1 0.6 dynamic_slice.6
  264.7 0.6 dynamic_slice.7
  (4 shorter events, 0.0 us)
Async XLA Ops:
  7.2 124.6 %all-gather.6.cloned.1.call-start = ((), (), s32[]{:S(2)}) async-start(), calls=%async_computation | async-start | bytes 8257536 | tf_op jit(solution)/shard_map/all_gather | solution.py:40
Sparse Core Ops, SparseCore 0:
  19.8 111.9 all-gather.5
where the time goes:
time: 275 us; the launch traced here: 274 us
  blocking collectives  166 us (60%)
  matrix products  43 us (16%)
  waiting for transfers between devices  36.2 us (13%)
  between operations  16.5 us (6%)
  other arithmetic  10.8 us (4%)
    dot_general x1, matrix products, body(): jnp.einsum('rd,vd->rv', lax.all_gather(full_rows, 'dp', axis=0, tiled=Tru...  43 us
    psum x1, blocking collectives, body(): lax.psum((total * jnp.exp(peak - top), picked), ('dp', 'vocab'))  40.8 us
    pmax x1, blocking collectives, body(): top = lax.pmax(peak, ('dp', 'vocab'))  38.4 us
    all_gather x1, waiting for transfers between devices, body(): lax.all_gather(full_rows, 'dp', axis=0, tiled=True)  36.2 us
    all_gather x1, blocking collectives, body(): lax.all_gather(response_mask, 'dp', axis=0, tiled=True)  21.4 us
    all_gather x1, blocking collectives, body(): lax.all_gather(rollout_logprobs, 'dp', axis=0, tiled=True)  18.8 us
    all_gather x1, blocking collectives, body(): lax.all_gather(advantages, 'dp', axis=0, tiled=True)  17.3 us
    all_gather x1, blocking collectives, body(): lax.all_gather(token_ids, 'dp', axis=0, tiled=True)  17.1 us
  transfers between devices with their start and end apart: 1, of which 1 were waited for; matrix products, arithmetic and copies ran while one was open for 0% of the time, Pallas kernels for 0%

commit v1 on v0

v1 whole, which is shorter than its diff:
```python
import functools

import jax
import jax.numpy as jnp
from jax import lax
from jax.experimental import pallas as pl
from jax.experimental.pallas import tpu as pltpu
from jax.sharding import PartitionSpec as P

MESH = pl.DeviceIdType.MESH
VMEM_BYTES = 64000 * 1024
LOW = -3.0e38


def shard_stats(logits, ids_block, columns):
    matched = columns[None, :] == ids_block[:, None]
    picked = jnp.sum(jnp.where(matched, logits, 0.0), axis=1)
    peak = jnp.max(logits, axis=1)
    total = jnp.sum(jnp.exp(logits - peak[:, None]), axis=1)
    return (peak, total, picked)


def token_terms(logp, rollout, advant, mask):
    weight = jnp.minimum(jnp.exp(logp - rollout), 2.0)
    counted = mask.astype(jnp.float32)
    loss_part = -jnp.sum(counted * weight * advant * logp)
    return (weight, loss_part, jnp.sum(counted))


def general_body(hidden_states, head_weight, token_ids, response_mask, rollout_logprobs, advantages):
    rows_local = token_ids.shape[0]
    vocab_local = head_weight.shape[0]
    offset = lax.axis_index(("dp", "vocab")) * vocab_local
    own_columns = lax.iota(jnp.int32, vocab_local) + offset
    own_start = lax.axis_index("dp") * rows_local
    gather = functools.partial(lax.all_gather, axis_name="dp", axis=0, tiled=True)
    all_ids, all_mask = gather(token_ids), gather(response_mask)
    all_rollout, all_advant = gather(rollout_logprobs), gather(advantages)
    full_rows = lax.all_gather(hidden_states, "vocab", axis=1, tiled=True)
    logits = jnp.einsum("rd,vd->rv", gather(full_rows), head_weight, preferred_element_type=jnp.float32)
    peak, total, picked = shard_stats(logits, all_ids, own_columns)
    top = lax.pmax(peak, ("dp", "vocab"))
    total_sum, picked_sum = lax.psum((total * jnp.exp(peak - top), picked), ("dp", "vocab"))
    logprob_all = picked_sum - (top + jnp.log(total_sum))
    own_logp = lax.dynamic_slice_in_dim(logprob_all, own_start, rows_local, 0)
    weight_all, loss_sum, count = token_terms(logprob_all, all_rollout, all_advant, all_mask)
    weight = lax.dynamic_slice_in_dim(weight_all, own_start, rows_local, 0)
    return (own_logp, weight, loss_sum / jnp.maximum(count, 1.0))


L, XA, XB, YA, YB, D0, D1, PL, PX, PY, PD = range(11)


def kernel(dp, nv, rows, feats, vt, tiles, x_hbm, w_hbm, side_ref, out_ref,
           h_ref, w_ref, logit_ref, m_ref, l_ref, p_ref, stat_ref, side_buf, fin_ref,
           recv, send, wsem, own_sem, side_recv, side_send, stat_recv, stat_send):
    chunks = dp // 2
    half = rows // 2
    cols = 2 * rows
    everyone = dp * nv
    g_me, v_me = lax.axis_index("dp"), lax.axis_index("vocab")
    me = g_me * nv + v_me
    z, x, y, k = g_me // 2, g_me % 2, v_me // 2, v_me % 2
    xn, yn, kn = 1 - x, 1 - y, 1 - k
    to_x = (g_me + 1 - 2 * x, v_me)
    to_y = (g_me, yn * 2 + k)
    to_p = (g_me, y * 2 + kn)
    to_z = ((g_me + 2) % dp, v_me)

    def wcopy(i):
        return pltpu.make_async_copy(w_hbm.at[pl.ds(pl.multiple_of(i * vt, 16), vt)], w_ref.at[i], wsem.at[i])

    def block(c, bx, by, bk, first=0, count=rows):
        return h_ref.at[c, pl.ds(pl.multiple_of(bx * rows + first, 16), count),
                        pl.ds(pl.multiple_of((by * 2 + bk) * feats, 128), feats)]

    own = block(z, x, y, k)
    own_copy = pltpu.make_async_copy(x_hbm, own, own_sem)
    own_copy.start()

    barrier = pltpu.get_barrier_semaphore()

    def greet(o, carry):
        t = (me + o) % everyone
        pl.semaphore_signal(barrier, inc=1, device_id=(t // nv, t % nv), device_id_type=MESH)
        return carry

    lax.fori_loop(1, everyone, greet, 0)
    lax.fori_loop(0, tiles, lambda i, a: (wcopy(i).start(), a)[1], 0)
    side_buf[g_me] = side_ref[...]
    own_copy.wait()
    pl.semaphore_wait(barrier, everyone - 1)

    def remote(ref, kind, t, to):
        return pltpu.make_async_remote_copy(
            src_ref=ref, dst_ref=ref, send_sem=send.at[kind, t], recv_sem=recv.at[kind, t],
            device_id=to, device_id_type=MESH)

    def came(ref, kind, t):
        pltpu.make_async_copy(ref, ref, recv.at[kind, t]).wait()

    def chunk_of(t):
        return (z - t + chunks) % chunks

    def line(t, wait):
        c = chunk_of(t)
        b = block(c, x, y, k)
        if wait:
            came(b, L, t)
        h0, h1 = block(c, x, y, k, 0, half), block(c, x, y, k, half, half)
        remote(h0, XA, t, to_x).start()
        remote(h1, YA, t, to_y).start()

        def onward():
            remote(b, L, t + 1, to_z).start()

        pl.when(t < chunks - 1)(onward)
        remote(h1, XB, t, to_x).start()
        remote(h0, YB, t, to_y).start()
        remote(b, PL, t, to_p).start()

    def relay(t):
        c = chunk_of(t)
        bx, by = block(c, xn, y, k, 0, half), block(c, x, yn, k, half, half)
        came(bx, XA, t)
        remote(bx, D0, t, to_y).start()
        came(by, YA, t)
        remote(by, D1, t, to_x).start()

    def across(t):
        c = chunk_of(t)
        came(block(c, xn, y, k, half, half), XB, t)
        remote(block(c, xn, y, k), PX, t, to_p).start()
        came(block(c, x, yn, k, 0, half), YB, t)
        remote(block(c, x, yn, k), PY, t, to_p).start()

    def corner(t):
        c = chunk_of(t)
        came(block(c, xn, yn, k, 0, half), D0, t)
        came(block(c, xn, yn, k, half, half), D1, t)
        remote(block(c, xn, yn, k), PD, t, to_p).start()

    def ready(t):
        c = chunk_of(t)
        came(block(c, x, y, kn), PL, t)
        came(block(c, xn, y, kn), PX, t)
        came(block(c, x, yn, kn), PY, t)
        came(block(c, xn, yn, kn), PD, t)

    line(0, False)

    def tell(o, carry):
        t = (g_me + o) % dp
        pltpu.make_async_remote_copy(
            src_ref=side_ref, dst_ref=side_buf.at[g_me], send_sem=side_send, recv_sem=side_recv,
            device_id=(t, v_me), device_id_type=MESH).start()
        return carry

    lax.fori_loop(1, dp, tell, 0)
    relay(0)
    if chunks > 1:
        line(1, True)
    across(0)
    corner(0)
    others = side_buf.at[pl.ds(0, dp - 1)]
    pltpu.make_async_copy(others, others, side_recv).wait()
    pltpu.make_async_copy(others, others, side_send).wait()
    logit_ref[1] = jnp.zeros((vt, cols), jnp.float32)

    sub = lax.broadcasted_iota(jnp.int32, (8, cols), 0)
    groups = vt // 8

    def epilogue(g):
        s, i = g // tiles, g % tiles
        slot = g % 2
        c = chunk_of(s)
        ids = jnp.concatenate([side_buf[2 * c, 0:1, :], side_buf[2 * c + 1, 0:1, :]], axis=1).astype(jnp.int32)
        rel = ids - (me * (vt * tiles) + i * vt) - sub
        first = jnp.full((8, cols), i, jnp.int32) == 0
        m_old = jnp.where(first, LOW, m_ref[...])
        tops = [m_old] + [None] * 3
        for j in range(groups):
            val = logit_ref[slot, 8 * j:8 * j + 8, :]
            q = j % 4
            tops[q] = val if tops[q] is None else jnp.maximum(tops[q], val)
        m_new = functools.reduce(jnp.maximum, [t for t in tops if t is not None])
        sums = [jnp.where(first, 0.0, l_ref[...]) * jnp.exp(m_old - m_new), jnp.zeros((8, cols), jnp.float32)]
        picks = [jnp.where(first, 0.0, p_ref[...]), jnp.zeros((8, cols), jnp.float32)]
        for j in range(groups):
            val = logit_ref[slot, 8 * j:8 * j + 8, :]
            q = j % 2
            sums[q] = sums[q] + jnp.exp(val - m_new)
            picks[q] = picks[q] + jnp.where(rel == 8 * j, val, 0.0)
        m_ref[...] = m_new
        l_ref[...] = sums[0] + sums[1]
        p_ref[...] = picks[0] + picks[1]

    def finish(s):
        c = chunk_of(s)
        m, l, p = m_ref[...], l_ref[...], p_ref[...]
        peak = jnp.max(m, axis=0, keepdims=True)
        total = jnp.sum(l * jnp.exp(m - peak), axis=0, keepdims=True)
        pick = jnp.sum(p, axis=0, keepdims=True)
        pad = jnp.zeros((2, rows), jnp.float32)
        stat_ref[me, c] = jnp.concatenate(
            [peak[:, :rows], peak[:, rows:], total[:, :rows], total[:, rows:],
             pick[:, :rows], pick[:, rows:], pad], axis=0)

    def spread(s):
        c = chunk_of(s)
        mine = stat_ref.at[me, c]

        def one(o, carry):
            t = (me + o) % everyone
            pltpu.make_async_remote_copy(
                src_ref=mine, dst_ref=mine, send_sem=stat_send, recv_sem=stat_recv,
                device_id=(t // nv, t % nv), device_id_type=MESH).start()
            return carry

        lax.fori_loop(1, everyone, one, 0)

    def step(g, carry):
        s, i = g // tiles, g % tiles
        slot = g % 2
        pl.when(s == 0)(lambda: wcopy(i).wait())
        pl.when(i == 0)(lambda: ready(s))

        def middle():
            relay(s + 1)
            pl.when(s + 2 < chunks)(lambda: line(s + 2, True))

        more = s + 1 < chunks
        pl.when((i == tiles // 3) & more)(middle)
        pl.when((i == (2 * tiles) // 3) & more)(lambda: across(s + 1))
        pl.when((i == tiles - 1) & more)(lambda: corner(s + 1))
        pl.when((i == 1) & (s > 0))(lambda: spread(s - 1))
        logit_ref[slot] = lax.dot_general(
            w_ref[i], h_ref[chunk_of(s)], (((1,), (1,)), ((), ())), preferred_element_type=jnp.float32)
        epilogue(jnp.where(g == 0, 1, g - 1))
        pl.when((i == 0) & (s > 0))(lambda: finish(s - 1))
        return carry

    last = chunks * tiles
    lax.fori_loop(0, last, step, 0)
    epilogue(last - 1)
    finish(chunks - 1)
    spread(chunks - 1)

    full, part = block(0, 0, 0, 0), block(0, 0, 0, 0, 0, half)

    def left(t, carry):
        for kind in (XA, XB, YA, YB, D0, D1):
            pltpu.make_async_copy(part, part, send.at[kind, t]).wait()
        for kind in (PL, PX, PY, PD):
            pltpu.make_async_copy(full, full, send.at[kind, t]).wait()
        pl.when(t > 0)(lambda: pltpu.make_async_copy(full, full, send.at[L, t]).wait())
        return carry

    lax.fori_loop(0, chunks, left, 0)
    rest = stat_ref.at[pl.ds(0, everyone - 1)]
    pltpu.make_async_copy(rest, rest, stat_recv).wait()
    pltpu.make_async_copy(rest, rest, stat_send).wait()

    loss_sum = jnp.zeros((1, rows), jnp.float32)
    count = jnp.zeros((1, rows), jnp.float32)
    for c in range(chunks):
        top = stat_ref[0, c]
        for d in range(1, everyone):
            top = jnp.maximum(top, stat_ref[d, c])
        total = jnp.zeros((2, rows), jnp.float32)
        pick = jnp.zeros((2, rows), jnp.float32)
        for d in range(everyone):
            t = stat_ref[d, c]
            total = total + t[2:4] * jnp.exp(t[0:2] - top[0:2])
            pick = pick + t[4:6]
        logp = pick - (top[0:2] + jnp.log(total))
        for r in range(2):
            g = 2 * c + r
            lp = logp[r:r + 1]
            mask, roll, adv = side_buf[g, 1:2, :], side_buf[g, 2:3, :], side_buf[g, 3:4, :]
            weight = jnp.minimum(jnp.exp(lp - roll), 2.0)
            loss_sum = loss_sum - mask * weight * adv * lp
            count = count + mask
            fin_ref[g, 0:1, :] = lp
            fin_ref[g, 1:2, :] = weight
    loss = jnp.sum(loss_sum, axis=1, keepdims=True) / jnp.maximum(jnp.sum(count, axis=1, keepdims=True), 1.0)
    out_ref[0:2, :] = fin_ref[g_me, 0:2, :]
    out_ref[2:8, :] = jnp.broadcast_to(loss, (6, rows))


def tile_rows(vocab_local):
    fits = [t for t in range(16, 545, 16) if vocab_local % t == 0]
    return max(fits) if fits else 0


def fused_body(dp, nv, vt, hidden_states, head_weight, token_ids, response_mask, rollout_logprobs, advantages):
    rows, feats = hidden_states.shape
    vocab_local, width = head_weight.shape
    chunks, tiles = dp // 2, vocab_local // vt
    side = jnp.stack([token_ids.astype(jnp.float32), response_mask.astype(jnp.float32),
                      rollout_logprobs, advantages] + [jnp.zeros_like(advantages)] * 4)
    any_spec = pl.BlockSpec(memory_space=pl.ANY)
    vmem_spec = pl.BlockSpec(memory_space=pltpu.VMEM)
    dma = pltpu.SemaphoreType.DMA
    out = pl.pallas_call(
        functools.partial(kernel, dp, nv, rows, feats, vt, tiles),
        out_shape=jax.ShapeDtypeStruct((8, rows), jnp.float32),
        in_specs=[any_spec, any_spec, vmem_spec],
        out_specs=vmem_spec,
        scratch_shapes=[
            pltpu.VMEM((chunks, 2 * rows, width), jnp.bfloat16),
            pltpu.VMEM((tiles, vt, width), jnp.bfloat16),
            pltpu.VMEM((2, vt, 2 * rows), jnp.float32),
            pltpu.VMEM((8, 2 * rows), jnp.float32),
            pltpu.VMEM((8, 2 * rows), jnp.float32),
            pltpu.VMEM((8, 2 * rows), jnp.float32),
            pltpu.VMEM((dp * nv, chunks, 8, rows), jnp.float32),
            pltpu.VMEM((dp, 8, rows), jnp.float32),
            pltpu.VMEM((dp, 8, rows), jnp.float32),
            dma((11, chunks)), dma((11, chunks)), dma((tiles,)), dma, dma, dma, dma, dma,
        ],
        compiler_params=pltpu.CompilerParams(
            collective_id=0, has_side_effects=True, vmem_limit_bytes=VMEM_BYTES),
    )(hidden_states, head_weight, side)
    return out[0], out[1], out[2, 0]


def solution(mesh):
    placed = (P("dp", "vocab"), P(("dp", "vocab"), None), P("dp"), P("dp"), P("dp"), P("dp"))
    dp, nv = mesh.shape["dp"], mesh.shape["vocab"]

    def body(hidden_states, head_weight, *rest):
        rows, feats = hidden_states.shape
        vt = tile_rows(head_weight.shape[0])
        held = 2 * (head_weight.size + rows * dp * head_weight.shape[1]) + 16 * vt * rows
        fits = (dp % 2 == 0 and dp > 2 and nv == 4 and vt > 0 and rows == 128 and feats % 128 == 0
                and held < VMEM_BYTES - (8 << 20))
        if fits:
            return fused_body(dp, nv, vt, hidden_states, head_weight, *rest)
        return general_body(hidden_states, head_weight, *rest)

    return jax.shard_map(
        body, mesh=mesh, in_specs=placed, out_specs=(P("dp"), P("dp"), P()), check_vma=False
    )
```

time: 275 us -> 84.5 us (0.31)
  blocking collectives: 166 us -> 0 us
  Pallas kernels: 0 us -> 79.1 us
  matrix products: 43 us -> 0 us
  waiting for transfers between devices: 36.2 us -> 0 us
  between operations: 16.5 us -> 0.64 us
  other arithmetic: 10.8 us -> 0.68 us
    all_gather x5 -> x0, blocking collectives: 87.1 us -> none  [the longest x1 21.4 us: body(): lax.all_gather(response_mask, 'dp', axis=0, tiled=True)]
    pallas_call x0 -> x1, Pallas kernels: none -> 79.1 us  [fused_body(): pl.pallas_call(functools.partial(kernel, dp, nv, rows, feats, vt, tiles),...]
    dot_general x1 -> x0, matrix products: 43 us -> none  [body(): jnp.einsum('rd,vd->rv', lax.all_gather(full_rows, 'dp', axis=0, tiled=Tru...]
    psum x1 -> x0, blocking collectives: 40.8 us -> none  [body(): lax.psum((total * jnp.exp(peak - top), picked), ('dp', 'vocab'))]
    pmax x1 -> x0, blocking collectives: 38.4 us -> none  [body(): top = lax.pmax(peak, ('dp', 'vocab'))]
    all_gather x1 -> x0, waiting for transfers between devices: 36.2 us -> none  [body(): lax.all_gather(full_rows, 'dp', axis=0, tiled=True)]
    reduce_sum x3 -> x0, other arithmetic: 10.7 us -> none  [the longest x1 9.52 us: shard_stats(): total = jnp.sum(jnp.exp(logits - peak[:, None]), axis=1)]
  transfers between devices with their start and end apart: 1 -> 0, of which waited for: 1 -> 0; matrix products, arithmetic and copies ran while one was open for 0% -> 0% of each run, Pallas kernels for 0% -> 0%
where the time goes in v1:
time: 84.5 us; the launch traced here: 84.2 us
  Pallas kernels  79.1 us (94%)
  local copies, waits for them, and re-layouts  3.74 us (4%)
    pallas_call x1, Pallas kernels, fused_body(): pl.pallas_call(functools.partial(kernel, dp, nv, rows, feats, vt, tiles),...  79.1 us

profile of v1, /device:TPU:0, one launch (start us, length us, event | category | flops | bytes accessed | tf_op | source)
XLA Modules:
  0.0 84.2 jit_solution(4494752967919932669)
XLA Ops:
  0.6 0.7 convert_bitcast_fusion
  1.3 1.3 %stack.23.side_ref = f32[8,128]{1,0:T(8,128)} concatenate(f32[1,128]{1,0:T(1,128)S(1)} %get-tuple-element.6, f32[1,128]{1,0:T(1,128)S(1)} %get-tuple-element.5, f32[1,128]{1,0:T(1,128)} %bitcast.11, f32[1,128]{1,0:T(1,128)} %bitcast.12, f32[4,128]{1,0:T(4,128)S(1)} %stack.22), dimensions={0} | concatenate | bytes 8192 | tf_op jit(solution)/shard_map/stack | solution.py:300
  2.6 79.1 %shard_map.85 = f32[8,128]{1,0:T(8,128)} custom-call(bf16[128,896]{1,0:T(8,128)(2,1)} %x_hbm.1, bf16[4752,3584]{1,0:T(8,128)(2,1)} %w_hbm.1, f32[8,128]{1,0:T(8,128)} %stack.23.side_ref), custom_call_target="tpu_custom_call" | custom-call | tf_op jit(solution)/shard_map/pallas_call | solution.py:305
  81.7 1.2 %slice.11 = f32[1,1]{1,0:T(1,128)} slice(f32[8,128]{1,0:T(8,128)} %shard_map.85), slice={[2:3], [0:1]} | slice | bytes 8 | tf_op jit(solution)/shard_map/slice | solution.py:325
  82.9 1.3 %slice_bitcast_fusion = (f32[128]{0:T(128)}, f32[128]{0:T(128)}) fusion(f32[8,128]{1,0:T(8,128)} %shard_map.85), kind=kLoop, calls=%fused_computation | loop fusion | bytes 2048 | tf_op jit(solution)/shard_map/squeeze | solution.py:325
  (1 shorter events, 0.0 us)

commit v2 on v1

--- a/solution.py
+++ b/solution.py
@@ -81,8 +81,8 @@
     barrier = pltpu.get_barrier_semaphore()
 
     def greet(o, carry):
-        t = (me + o) % everyone
-        pl.semaphore_signal(barrier, inc=1, device_id=(t // nv, t % nv), device_id_type=MESH)
+        t = lax.rem(me + o, everyone)
+        pl.semaphore_signal(barrier, inc=1, device_id=(lax.div(t, nv), lax.rem(t, nv)), device_id_type=MESH)
         return carry
 
     lax.fori_loop(1, everyone, greet, 0)
@@ -150,7 +150,7 @@
     line(0, False)
 
     def tell(o, carry):
-        t = (g_me + o) % dp
+        t = lax.rem(g_me + o, dp)
         pltpu.make_async_remote_copy(
             src_ref=side_ref, dst_ref=side_buf.at[g_me], send_sem=side_send, recv_sem=side_recv,
             device_id=(t, v_me), device_id_type=MESH).start()
@@ -158,9 +158,9 @@
 
     lax.fori_loop(1, dp, tell, 0)
     relay(0)
+    across(0)
     if chunks > 1:
         line(1, True)
-    across(0)
     corner(0)
     others = side_buf.at[pl.ds(0, dp - 1)]
     pltpu.make_async_copy(others, others, side_recv).wait()
@@ -211,10 +211,10 @@
         mine = stat_ref.at[me, c]
 
         def one(o, carry):
-            t = (me + o) % everyone
+            t = lax.rem(me + o, everyone)
             pltpu.make_async_remote_copy(
                 src_ref=mine, dst_ref=mine, send_sem=stat_send, recv_sem=stat_recv,
-                device_id=(t // nv, t % nv), device_id_type=MESH).start()
+                device_id=(lax.div(t, nv), lax.rem(t, nv)), device_id_type=MESH).start()
             return carry
 
         lax.fori_loop(1, everyone, one, 0)
@@ -289,7 +289,7 @@
 
 
 def tile_rows(vocab_local):
-    fits = [t for t in range(16, 545, 16) if vocab_local % t == 0]
+    fits = [t for t in range(16, 1601, 16) if vocab_local % t == 0]
     return max(fits) if fits else 0
 
 

time: 84.5 us -> 79.6 us (0.942)
  Pallas kernels: 79.1 us -> 74.2 us
    pallas_call x1, Pallas kernels: 79.1 us -> 74.2 us  [fused_body(): pl.pallas_call(functools.partial(kernel, dp, nv, rows, feats, vt, tiles),...]
where the time goes in v2:
time: 79.6 us; the launch traced here: 79.3 us
  Pallas kernels  74.2 us (93%)
  local copies, waits for them, and re-layouts  3.74 us (5%)
    pallas_call x1, Pallas kernels, fused_body(): pl.pallas_call(functools.partial(kernel, dp, nv, rows, feats, vt, tiles),...  74.2 us

profile of v2, /device:TPU:0, one launch (start us, length us, event | category | flops | bytes accessed | tf_op | source)
XLA Modules:
  0.0 79.3 jit_solution(11973483396093062137)
XLA Ops:
  0.6 0.7 convert_bitcast_fusion
  1.3 1.3 %stack.23.side_ref = f32[8,128]{1,0:T(8,128)} concatenate(f32[1,128]{1,0:T(1,128)S(1)} %get-tuple-element.6, f32[1,128]{1,0:T(1,128)S(1)} %get-tuple-element.5, f32[1,128]{1,0:T(1,128)} %bitcast.11, f32[1,128]{1,0:T(1,128)} %bitcast.12, f32[4,128]{1,0:T(4,128)S(1)} %stack.22), dimensions={0} | concatenate | bytes 8192 | tf_op jit(solution)/shard_map/stack | solution.py:300
  2.6 74.2 %shard_map.85 = f32[8,128]{1,0:T(8,128)} custom-call(bf16[128,896]{1,0:T(8,128)(2,1)} %x_hbm.1, bf16[4752,3584]{1,0:T(8,128)(2,1)} %w_hbm.1, f32[8,128]{1,0:T(8,128)} %stack.23.side_ref), custom_call_target="tpu_custom_call" | custom-call | tf_op jit(solution)/shard_map/pallas_call | solution.py:305
  76.8 1.2 %slice.11 = f32[1,1]{1,0:T(1,128)} slice(f32[8,128]{1,0:T(8,128)} %shard_map.85), slice={[2:3], [0:1]} | slice | bytes 8 | tf_op jit(solution)/shard_map/slice | solution.py:325
  78.0 1.3 %slice_bitcast_fusion = (f32[128]{0:T(128)}, f32[128]{0:T(128)}) fusion(f32[8,128]{1,0:T(8,128)} %shard_map.85), kind=kLoop, calls=%fused_computation | loop fusion | bytes 2048 | tf_op jit(solution)/shard_map/squeeze | solution.py:325
  (1 shorter events, 0.0 us)
